TPU v7x, 32 devices: a whole 2x2x4 slice. The times are simulated.
32 devices in a mesh: sx: 4 (over x, core), sy: 2 (over y), px: 4 (over z).
Axes of the slice: x: 2, y: 2, z: 4, core: 2. Of those that a mesh axis runs over, the one named last changes fastest.
Arguments:
- patterns: bfloat16 [64, 64, 9216], P('sx', 'sy', 'px'), may hold values from -6 to 6
- basis: bfloat16 [9216, 256], P('px', ('sx', 'sy')), may hold values from -0.375 to 0.375
- valid: int32 [64, 64], P('sx', 'sy'), may hold values 0 or 1
- strength: float32 [64, 64], P('sx', 'sy'), may hold values from 0.25 to 2
Outputs:
- denoised: bfloat16 [64, 64, 9216], P('sx', 'sy', 'px')
Inputs may be any that keep to these rules, and one draw needn't show every extreme that they name: `valid`: 1 marks an on-sample scan position, 0 an off-sample one.
All inputs are finite; a program needn't handle non-finite values. No bound on the sum of `valid` on one device may be relied on, other than what follows from the above.
Results may differ from a plain program's by a relative error of at most 0.0089.
Values may be sent and summed in bfloat16 or wider, within the bound.
No kernel may reach another device: no remote copies, remote signals or barrier semaphores. Data moves between devices by JAX's collectives and lax.ppermute only.
A program may use at most 64 MiB of HBM per device.

v0:
```python
import jax
import jax.numpy as jnp
from jax import lax
from jax.sharding import PartitionSpec as P

PIX = 9216
RADIUS = 3


def extended(array, sides, width):
    for axis, dim in sides:
        count, length = (lax.axis_size(axis), array.shape[dim])
        up = [(i, (i + 1) % count) for i in range(count - 1)]
        down = [(j, i) for i, j in up]
        last = lax.slice_in_dim(array, length - width, length, axis=dim)
        initial = lax.slice_in_dim(array, 0, width, axis=dim)
        before = lax.ppermute(last, axis, up)
        after = lax.ppermute(initial, axis, down)
        array = jnp.concatenate([before, array, after], axis=dim)
    return array


def neighbour_steps():
    steps = []
    for row_step in range(-RADIUS, RADIUS + 1):
        for col_step in range(-RADIUS, RADIUS + 1):
            if row_step != 0 or col_step != 0:
                steps.append((row_step, col_step))
    return steps


def squared_gaps(center, padded):
    rows, cols = (center.shape[0], center.shape[1])
    gaps = []
    for row_step, col_step in neighbour_steps():
        other = padded[
            RADIUS + row_step : RADIUS + row_step + rows,
            RADIUS + col_step : RADIUS + col_step + cols,
        ]
        differ = center - other
        gaps.append(jnp.sum(differ * differ, axis=-1))
    return jnp.stack(gaps)


def blend(center, padded, mask_pad, gaps, strength):
    rows, cols = (center.shape[0], center.shape[1])
    factor = 1.0 / (2.0 * PIX * strength)
    numerator = center
    total = jnp.ones((rows, cols), jnp.float32)
    for index, (row_step, col_step) in enumerate(neighbour_steps()):
        other = padded[
            RADIUS + row_step : RADIUS + row_step + rows,
            RADIUS + col_step : RADIUS + col_step + cols,
        ]
        mask_other = mask_pad[
            RADIUS + row_step : RADIUS + row_step + rows,
            RADIUS + col_step : RADIUS + col_step + cols,
        ]
        weight = mask_other * jnp.exp(-gaps[index] * factor)
        numerator = numerator + weight[:, :, None] * other
        total = total + weight
    return numerator / total[:, :, None]


def extend(coeffs, mask_full):
    return (
        extended(coeffs, (("sx", 0), ("sy", 1)), RADIUS),
        extended(mask_full, (("sx", 0), ("sy", 1)), RADIUS),
    )


def on_device(patterns, basis, valid, strength):
    cells_x, cells_y, pixels = patterns.shape
    flat = patterns.reshape(cells_x * cells_y, pixels)
    whole_basis = lax.all_gather(basis, ("sx", "sy"), axis=1, tiled=True)
    partial_value = jnp.dot(flat, whole_basis, preferred_element_type=jnp.float32)
    partial_value = partial_value.reshape(cells_x, cells_y, partial_value.shape[1])
    mask_full = valid.astype(jnp.float32)
    coeffs = lax.psum(partial_value, "px")
    padded, mask_pad = extend(coeffs, mask_full)
    gaps = squared_gaps(coeffs, padded)
    average = blend(coeffs, padded, mask_pad, gaps, strength).astype(jnp.bfloat16)
    avg_flat = average.reshape(cells_x * cells_y, average.shape[2])
    rebuilt = lax.dot_general(
        avg_flat, whole_basis, (((1,), (1,)), ((), ())), preferred_element_type=jnp.float32
    )
    return rebuilt.astype(jnp.bfloat16).reshape(cells_x, cells_y, pixels)


def solution(mesh):
    return jax.shard_map(
        on_device,
        mesh=mesh,
        in_specs=(P("sx", "sy", "px"), P("px", ("sx", "sy")), P("sx", "sy"), P("sx", "sy")),
        out_specs=P("sx", "sy", "px"),
        check_vma=False,
    )
```

profile of v0, /device:TPU:1, one launch (start us, length us, event | category | flops | bytes accessed | tf_op | source)
XLA Modules:
  0.0 117.6 jit_solution(7627593339896749223)
XLA Ops:
  6.5 0.0 copy-start
  6.5 0.0 all-gather.2.cloned.1.call-start
  6.5 0.7 all-gather.2.cloned.1.call-update
  7.3 0.0 copy-start.4
  7.3 0.0 all-reduce.2.cloned.1.call-start
  7.3 28.3 %all-gather.2.cloned.1.call-done = bf16[2304,256]{0,1:T(8,128)(2,1)} async-done(((bf16[2304,32]{0,1:T(8,128)(2,1)}), bf16[2304,256]{0,1:T(8,128)(2,1)}) %all-gather.2.cloned.1.call-update) | async-done | bytes 1179664 | tf_op jit(solution)/shard_map/all_gather | solution.py:75
  35.6 0.0 copy-done
  35.6 2.9 %fusion = f32[16,32,256]{2,1,0:T(8,128)} fusion(bf16[16,32,2304]{2,1,0:T(8,128)(2,1)S(1)} %copy-done, bf16[2304,256]{0,1:T(8,128)(2,1)} %all-gather.2.cloned.1.call-done), kind=kOutput, calls=%fused_computation.81 | convolution fusion | flops 603979776 | bytes 4063232 | tf_op jit(solution)/shard_map/dot_general | solution.py:76
  38.5 0.0 all-reduce.2.cloned.1.call-update
  38.5 0.0 copy-done.4
  38.6 3.3 %collective-permute-start = (f32[3,32]{1,0:T(4,128)S(1)}, f32[3,32]{1,0:T(4,128)S(1)}, u32[]{:S(2)}, u32[]{:S(2)}) collective-permute-start(f32[3,32]{1,0:T(4,128)S(1)} %get-tuple-element.124), channel_id=1, source_target_pairs={{0,8},{8,16},{16,24},{1,9},{9,17},{17,25},{2,10},{10,18},{18,26},{... | collective-permute-start | bytes 1160 | tf_op jit(solution)/shard_map/ppermute | solution.py:17
  41.8 1.9 %collective-permute-start.1 = (f32[3,32]{1,0:T(4,128)S(1)}, f32[3,32]{1,0:T(4,128)S(1)}, u32[]{:S(2)}, u32[]{:S(2)}) collective-permute-start(f32[3,32]{1,0:T(4,128)S(1)} %get-tuple-element.125), channel_id=1, source_target_pairs={{8,0},{16,8},{24,16},{9,1},{17,9},{25,17},{10,2},{18,10},{26,18},{... | collective-permute-start | bytes 1160 | tf_op jit(solution)/shard_map/ppermute | solution.py:18
  43.8 0.0 collective-permute-done
  43.8 3.4 %collective-permute-done.1 = f32[3,32]{1,0:T(4,128)S(1)} collective-permute-done((f32[3,32]{1,0:T(4,128)S(1)}, f32[3,32]{1,0:T(4,128)S(1)}, u32[]{:S(2)}, u32[]{:S(2)}) %collective-permute-start.1) | collective-permute-done | bytes 416 | tf_op jit(solution)/shard_map/ppermute | solution.py:18
  47.1 28.8 %all-reduce.2.cloned.1.call-done = f32[16,32,256]{2,1,0:T(8,128)} async-done(((f32[16,32,256]{2,1,0:T(8,128)}), f32[16,32,256]{2,1,0:T(8,128)}) %all-reduce.2.cloned.1.call-update) | async-done | bytes 524304 | tf_op jit(solution)/shard_map/psum | solution.py:79
  76.0 0.0 copy-start.1
  76.0 1.0 fusion.59
  77.0 4.6 %collective-permute-start.3 = (f32[3,32,256]{2,1,0:T(8,128)S(1)}, f32[3,32,256]{2,1,0:T(8,128)S(1)}, u32[]{:S(2)}, u32[]{:S(2)}) collective-permute-start(f32[3,32,256]{2,1,0:T(8,128)S(1)} %get-tuple-element.116), channel_id=1, source_target_pairs={{0,8},{8,16},{16,24},{1,9},{9,17},{17,25},{2,10},{10,18},{18,26},{... | collective-permute-start | bytes 294920 | tf_op jit(solution)/shard_map/ppermute | solution.py:17
  81.6 0.1 fusion.60
  81.7 3.1 %collective-permute-start.2 = (f32[22,3]{1,0:T(8,128)S(1)}, f32[22,3]{1,0:T(8,128)S(1)}, u32[]{:S(2)}, u32[]{:S(2)}) collective-permute-start(f32[22,3]{1,0:T(8,128)S(1)} %get-tuple-element.123), channel_id=1, source_target_pairs={{0,4},{1,5},{2,6},{3,7},{8,12},{9,13},{10,14},{11,15},{16,20},{17,... | collective-permute-start | bytes 800 | tf_op jit(solution)/shard_map/ppermute | solution.py:17
  84.7 1.3 %collective-permute-start.6 = (f32[22,3]{1,0:T(8,128)S(1)}, f32[22,3]{1,0:T(8,128)S(1)}, u32[]{:S(2)}, u32[]{:S(2)}) collective-permute-start(f32[22,3]{1,0:T(8,128)S(1)} %get-tuple-element.122), channel_id=1, source_target_pairs={{4,0},{5,1},{6,2},{7,3},{12,8},{13,9},{14,10},{15,11},{20,16},{21,... | collective-permute-start | bytes 800 | tf_op jit(solution)/shard_map/ppermute | solution.py:18
  86.0 1.9 %collective-permute-start.4 = (f32[3,32,256]{2,1,0:T(8,128)S(1)}, f32[3,32,256]{2,1,0:T(8,128)S(1)}, u32[]{:S(2)}, u32[]{:S(2)}) collective-permute-start(f32[3,32,256]{2,1,0:T(8,128)S(1)} %get-tuple-element.117), channel_id=1, source_target_pairs={{8,0},{16,8},{24,16},{9,1},{17,9},{25,17},{10,2},{18,10},{26,18},{... | collective-permute-start | bytes 294920 | tf_op jit(solution)/shard_map/ppermute | solution.py:18
  88.0 0.0 collective-permute-done.3
  88.0 1.2 constant_dynamic-update-slice_fusion.1
  89.2 2.8 %collective-permute-done.4 = f32[3,32,256]{2,1,0:T(8,128)S(1)} collective-permute-done((f32[3,32,256]{2,1,0:T(8,128)S(1)}, f32[3,32,256]{2,1,0:T(8,128)S(1)}, u32[]{:S(2)}, u32[]{:S(2)}) %collective-permute-start.4) | collective-permute-done | bytes 98336 | tf_op jit(solution)/shard_map/ppermute | solution.py:18
  92.0 1.3 %collective-permute-start.7 = (f32[22,3,256]{2,1,0:T(4,128)S(1)}, f32[22,3,256]{2,1,0:T(4,128)S(1)}, u32[]{:S(2)}, u32[]{:S(2)}) collective-permute-start(f32[22,3,256]{2,1,0:T(4,128)S(1)} %get-tuple-element.111), channel_id=1, source_target_pairs={{4,0},{5,1},{6,2},{7,3},{12,8},{13,9},{14,10},{15,11},{20,16},{21,... | collective-permute-start | bytes 202760 | tf_op jit(solution)/shard_map/ppermute | solution.py:18
  93.3 0.0 collective-permute-done.2
  93.3 0.0 collective-permute-done.6
  93.4 0.1 pad_maximum_fusion.3
  93.4 4.0 %collective-permute-start.5 = (f32[22,3,256]{2,1,0:T(4,128)S(1)}, f32[22,3,256]{2,1,0:T(4,128)S(1)}, u32[]{:S(2)}, u32[]{:S(2)}) collective-permute-start(f32[22,3,256]{2,1,0:T(4,128)S(1)} %get-tuple-element.112), channel_id=1, source_target_pairs={{0,4},{1,5},{2,6},{3,7},{8,12},{9,13},{10,14},{11,15},{16,20},{17,... | collective-permute-start | bytes 202760 | tf_op jit(solution)/shard_map/ppermute | solution.py:17
  97.4 0.0 collective-permute-done.7
  97.4 0.0 copy-done.1
  97.4 1.0 multiply_reduce_fusion.42
  98.4 1.0 multiply_reduce_fusion.43
  99.4 0.0 collective-permute-done.5
  99.4 1.1 multiply_reduce_fusion.46
  100.6 1.1 multiply_reduce_fusion.47
  101.7 0.0 copy-start.3
  101.7 1.2 %multiply_reduce_fusion.45 = (f32[16,32]{1,0:T(8,128)S(1)}, f32[16,32]{1,0:T(8,128)S(1)}, f32[16,32]{1,0:T(8,128)S(1)}, f32[16,32]{1,0:T(8,128)S(1)}, f32[16,32]...) fusion(f32[16,32,256]{2,1,0:T(8,128)S(1)} %copy-done.1, ...), kind=kLoop, calls=%fused_computation.171 | loop fusion | flops 5498880 | bytes 4550656 | tf_op jit(solution)/shard_map/reduce_sum | solution.py:41
  102.9 0.0 copy-done.3
  102.9 0.2 add_add_fusion
  103.1 0.0 copy-start.2
  103.1 5.4 %divide_convert_fusion = bf16[16,32,256]{2,1,0:T(8,128)(2,1)S(1)} fusion(f32[16,32,256]{2,1,0:T(8,128)S(1)} %copy-done.1, f32[19,32,256]{2,1,0:T(8,128)S(1)} %constant_dynamic-update-slice_fusion.5, f32[19,32,256]{2,1,0:T(8,128)S(1)} %get-tuple-element.115, f32[22,32,256]{2,1,0:T(8,128)S(1)} %constant_dynamic-update-slice_fusion, ...), kind=kLoop, calls=%fused_computation.125 | loop fusion | flops 18350080 | bytes 4888576 | tf_op jit(solution)/shard_map/convert_element_type | solution.py:82
  108.6 0.0 copy-done.2
  108.6 2.2 %convolution_convert_fusion = bf16[512,2304]{1,0:T(8,128)(2,1)} fusion(bf16[512,256]{1,0:T(8,128)(2,1)S(1)} %bitcast.8, bf16[2304,256]{0,1:T(8,128)(2,1)S(1)} %copy-done.2), kind=kOutput, calls=%fused_computation.40 | convolution fusion | flops 605159424 | bytes 3801088 | tf_op jit(solution)/shard_map/dot_general | solution.py:84
  (7 shorter events, 0.1 us)
Async XLA Ops:
  6.5 29.1 %copy-start = (bf16[16,32,2304]{2,1,0:T(8,128)(2,1)S(1)}, bf16[16,32,2304]{2,1,0:T(8,128)(2,1)}, u32[]{:S(2)}) copy-start(bf16[16,32,2304]{2,1,0:T(8,128)(2,1)} %param.4) | copy-start | bytes 7077892
  6.5 29.1 %all-gather.2.cloned.1.call-start = ((), (), s32[]{:S(2)}) async-start(), calls=%async_computation | async-start | bytes 1327104 | tf_op jit(solution)/shard_map/all_gather | solution.py:75
  7.3 31.3 %copy-start.4 = (s32[16,32]{1,0:T(8,128)S(1)}, s32[16,32]{1,0:T(8,128)}, u32[]{:S(2)}) copy-start(s32[16,32]{1,0:T(8,128)} %param.6) | copy-start | bytes 6148
  7.3 68.7 %all-reduce.2.cloned.1.call-start = ((), (), s32[]{:S(2)}) async-start(), calls=%async_computation.1 | async-start | bytes 1048576 | tf_op jit(solution)/shard_map/psum | solution.py:79
  38.6 5.2 %collective-permute-start = (f32[3,32]{1,0:T(4,128)S(1)}, f32[3,32]{1,0:T(4,128)S(1)}, u32[]{:S(2)}, u32[]{:S(2)}) collective-permute-start(f32[3,32]{1,0:T(4,128)S(1)} %get-tuple-element.124), channel_id=1, source_target_pairs={{0,8},{8,16},{16,24},{1,9},{9,17},{17,25},{2,10},{10,18},{18,26},{... | collective-permute-start | bytes 1160 | tf_op jit(solution)/shard_map/ppermute | solution.py:17
  41.8 5.3 %collective-permute-start.1 = (f32[3,32]{1,0:T(4,128)S(1)}, f32[3,32]{1,0:T(4,128)S(1)}, u32[]{:S(2)}, u32[]{:S(2)}) collective-permute-start(f32[3,32]{1,0:T(4,128)S(1)} %get-tuple-element.125), channel_id=1, source_target_pairs={{8,0},{16,8},{24,16},{9,1},{17,9},{25,17},{10,2},{18,10},{26,18},{... | collective-permute-start | bytes 1160 | tf_op jit(solution)/shard_map/ppermute | solution.py:18
  76.0 21.5 %copy-start.1 = (f32[16,32,256]{2,1,0:T(8,128)S(1)}, f32[16,32,256]{2,1,0:T(8,128)}, u32[]{:S(2)}) copy-start(f32[16,32,256]{2,1,0:T(8,128)} %all-reduce.2.cloned.1.call-done) | copy-start | bytes 1572868
  77.0 11.0 %collective-permute-start.3 = (f32[3,32,256]{2,1,0:T(8,128)S(1)}, f32[3,32,256]{2,1,0:T(8,128)S(1)}, u32[]{:S(2)}, u32[]{:S(2)}) collective-permute-start(f32[3,32,256]{2,1,0:T(8,128)S(1)} %get-tuple-element.116), channel_id=1, source_target_pairs={{0,8},{8,16},{16,24},{1,9},{9,17},{17,25},{2,10},{10,18},{18,26},{... | collective-permute-start | bytes 294920 | tf_op jit(solution)/shard_map/ppermute | solution.py:17
  81.7 11.7 %collective-permute-start.2 = (f32[22,3]{1,0:T(8,128)S(1)}, f32[22,3]{1,0:T(8,128)S(1)}, u32[]{:S(2)}, u32[]{:S(2)}) collective-permute-start(f32[22,3]{1,0:T(8,128)S(1)} %get-tuple-element.123), channel_id=1, source_target_pairs={{0,4},{1,5},{2,6},{3,7},{8,12},{9,13},{10,14},{11,15},{16,20},{17,... | collective-permute-start | bytes 800 | tf_op jit(solution)/shard_map/ppermute | solution.py:17
  84.7 8.6 %collective-permute-start.6 = (f32[22,3]{1,0:T(8,128)S(1)}, f32[22,3]{1,0:T(8,128)S(1)}, u32[]{:S(2)}, u32[]{:S(2)}) collective-permute-start(f32[22,3]{1,0:T(8,128)S(1)} %get-tuple-element.122), channel_id=1, source_target_pairs={{4,0},{5,1},{6,2},{7,3},{12,8},{13,9},{14,10},{15,11},{20,16},{21,... | collective-permute-start | bytes 800 | tf_op jit(solution)/shard_map/ppermute | solution.py:18
  86.0 5.9 %collective-permute-start.4 = (f32[3,32,256]{2,1,0:T(8,128)S(1)}, f32[3,32,256]{2,1,0:T(8,128)S(1)}, u32[]{:S(2)}, u32[]{:S(2)}) collective-permute-start(f32[3,32,256]{2,1,0:T(8,128)S(1)} %get-tuple-element.117), channel_id=1, source_target_pairs={{8,0},{16,8},{24,16},{9,1},{17,9},{25,17},{10,2},{18,10},{26,18},{... | collective-permute-start | bytes 294920 | tf_op jit(solution)/shard_map/ppermute | solution.py:18
  92.0 5.4 %collective-permute-start.7 = (f32[22,3,256]{2,1,0:T(4,128)S(1)}, f32[22,3,256]{2,1,0:T(4,128)S(1)}, u32[]{:S(2)}, u32[]{:S(2)}) collective-permute-start(f32[22,3,256]{2,1,0:T(4,128)S(1)} %get-tuple-element.111), channel_id=1, source_target_pairs={{4,0},{5,1},{6,2},{7,3},{12,8},{13,9},{14,10},{15,11},{20,16},{21,... | collective-permute-start | bytes 202760 | tf_op jit(solution)/shard_map/ppermute | solution.py:18
  93.4 6.0 %collective-permute-start.5 = (f32[22,3,256]{2,1,0:T(4,128)S(1)}, f32[22,3,256]{2,1,0:T(4,128)S(1)}, u32[]{:S(2)}, u32[]{:S(2)}) collective-permute-start(f32[22,3,256]{2,1,0:T(4,128)S(1)} %get-tuple-element.112), channel_id=1, source_target_pairs={{0,4},{1,5},{2,6},{3,7},{8,12},{9,13},{10,14},{11,15},{16,20},{17,... | collective-permute-start | bytes 202760 | tf_op jit(solution)/shard_map/ppermute | solution.py:17
  101.7 1.2 %copy-start.3 = (f32[16,32]{1,0:T(8,128)S(1)}, f32[16,32]{1,0:T(8,128)}, u32[]{:S(2)}) copy-start(f32[16,32]{1,0:T(8,128)} %param.7) | copy-start | bytes 6148
  103.1 5.5 %copy-start.2 = (bf16[2304,256]{0,1:T(8,128)(2,1)S(1)}, bf16[2304,256]{0,1:T(8,128)(2,1)}, u32[]{:S(2)}) copy-start(bf16[2304,256]{0,1:T(8,128)(2,1)} %all-gather.2.cloned.1.call-done) | copy-start | bytes 3538948
Sparse Core Ops, SparseCore 0:
  9.2 26.3 all-gather.1
  38.6 37.2 all-reduce.1
where the time goes:
time: 118 us
  waiting for transfers between devices  64.1 us (54%)
  starting transfers between devices  21.4 us (18%)
  between operations  13.7 us (12%)
  other arithmetic  11.1 us (9%)
  matrix products  5.06 us (4%)
  local copies, waits for them, and re-layouts  2.33 us (2%)
    psum x1, waiting for transfers between devices, on_device(): coeffs = lax.psum(partial_value, 'px')  28.8 us
    all_gather x1, waiting for transfers between devices, on_device(): whole_basis = lax.all_gather(basis, ('sx', 'sy'), axis=1, tiled=True)  28.3 us
    ppermute x4, starting transfers between devices, extended(): before = lax.ppermute(last, axis, up)  14.9 us
    ppermute x4, starting transfers between devices, extended(): after = lax.ppermute(initial, axis, down)  6.43 us
    ppermute x4, waiting for transfers between devices, extended(): after = lax.ppermute(initial, axis, down)  6.18 us
    convert_element_type x1, other arithmetic, on_device(): blend(coeffs, padded, mask_pad, gaps, strength).astype(jnp.bfloat16)  5.44 us
    reduce_sum x5, other arithmetic, squared_gaps(): gaps.append(jnp.sum(differ * differ, axis=-1))  5.39 us
    dot_general x1, matrix products, on_device(): jnp.dot(flat, whole_basis, preferred_element_type=jnp.float32)  2.87 us
  transfers between devices with their start and end apart: 10, of which 4 were waited for; matrix products, arithmetic and copies ran while one was open for 3% of the time, Pallas kernels for 0%

commit v1 on v0

--- a/solution.py
+++ b/solution.py
@@ -1,3 +1,4 @@
+import functools
 import jax
 import jax.numpy as jnp
 from jax import lax
@@ -5,6 +6,28 @@
 
 PIX = 9216
 RADIUS = 3
+
+
+def recover_group(target, which_axis):
+    world = jax.lax.axis_size(which_axis)
+
+    def lay_the_figure(e_next, oldest):
+        if oldest >= world:
+            return e_next
+        next_value = lay_the_figure(
+            e_next
+            + jax.lax.ppermute(
+                e_next, axis_name=which_axis, perm=tuple(((dd, dd ^ oldest) for dd in range(world)))
+            ),
+            2 * oldest,
+        )
+        return next_value
+
+    inter = lay_the_figure(target, 1)
+    return inter
+
+
+post_shards = functools.partial(recover_group, which_axis="px")
 
 
 def extended(array, sides, width):
@@ -76,7 +99,7 @@
     partial_value = jnp.dot(flat, whole_basis, preferred_element_type=jnp.float32)
     partial_value = partial_value.reshape(cells_x, cells_y, partial_value.shape[1])
     mask_full = valid.astype(jnp.float32)
-    coeffs = lax.psum(partial_value, "px")
+    coeffs = post_shards(partial_value)
     padded, mask_pad = extend(coeffs, mask_full)
     gaps = squared_gaps(coeffs, padded)
     average = blend(coeffs, padded, mask_pad, gaps, strength).astype(jnp.bfloat16)

time: 118 us -> 115 us (0.975)
  waiting for transfers between devices: 64.1 us -> 61.5 us
  starting transfers between devices: 21.4 us -> 23.9 us
  local copies, waits for them, and re-layouts: 2.33 us -> 0.11 us
    psum x1 -> x0, waiting for transfers between devices: 28.8 us -> none  [on_device(): coeffs = lax.psum(partial_value, 'px')]
    ppermute x0 -> x2, waiting for transfers between devices: none -> 25.6 us  [lay_the_figure(): jax.lax.ppermute(e_next, axis_name=which_axis, perm=tuple(((dd, dd ^ olde...]
    ppermute x0 -> x2, starting transfers between devices: none -> 3.46 us  [lay_the_figure(): jax.lax.ppermute(e_next, axis_name=which_axis, perm=tuple(((dd, dd ^ olde...]
    reduce_sum x5 -> x3, other arithmetic: 5.39 us -> 5.03 us  [squared_gaps(): gaps.append(jnp.sum(differ * differ, axis=-1))]
  transfers between devices with their start and end apart: 10 -> 11, of which waited for: 4 -> 6; matrix products, arithmetic and copies ran while one was open for 3% -> 0% of each run, Pallas kernels for 0% -> 0%
where the time goes in v1:
time: 115 us; the launch traced here: 114 us
  waiting for transfers between devices  61.5 us (53%)
  starting transfers between devices  23.9 us (21%)
  between operations  13.6 us (12%)
  other arithmetic  10.9 us (9%)
  matrix products  4.26 us (4%)
    all_gather x1, waiting for transfers between devices, on_device(): whole_basis = lax.all_gather(basis, ('sx', 'sy'), axis=1, tiled=True)  28.4 us
    ppermute x2, waiting for transfers between devices, lay_the_figure(): jax.lax.ppermute(e_next, axis_name=which_axis, perm=tuple(((dd, dd ^ olde...  25.6 us
    ppermute x4, starting transfers between devices, extended(): before = lax.ppermute(last, axis, up)  14.1 us
    ppermute x4, waiting for transfers between devices, extended(): after = lax.ppermute(initial, axis, down)  6.7 us
    ppermute x4, starting transfers between devices, extended(): after = lax.ppermute(initial, axis, down)  6.42 us
    convert_element_type x1, other arithmetic, on_device(): blend(coeffs, padded, mask_pad, gaps, strength).astype(jnp.bfloat16)  5.27 us
    reduce_sum x3, other arithmetic, squared_gaps(): gaps.append(jnp.sum(differ * differ, axis=-1))  5.03 us
    ppermute x2, starting transfers between devices, lay_the_figure(): jax.lax.ppermute(e_next, axis_name=which_axis, perm=tuple(((dd, dd ^ olde...  3.46 us
  transfers between devices with their start and end apart: 11, of which 6 were waited for; matrix products, arithmetic and copies ran while one was open for 0% of the time, Pallas kernels for 0%

profile of v1, /device:TPU:1, one launch (start us, length us, event | category | flops | bytes accessed | tf_op | source)
XLA Modules:
  0.0 114.4 jit_solution(12512100017574466511)
XLA Ops:
  6.5 0.0 copy-start
  6.5 0.0 all-gather.2.cloned.1.call-start
  6.5 0.7 all-gather.2.cloned.1.call-update
  7.3 0.0 copy-start.3
  7.3 28.4 %all-gather.2.cloned.1.call-done = bf16[2304,256]{0,1:T(8,128)(2,1)} async-done(((bf16[2304,32]{0,1:T(8,128)(2,1)}), bf16[2304,256]{0,1:T(8,128)(2,1)}) %all-gather.2.cloned.1.call-update) | async-done | bytes 1179664 | tf_op jit(solution)/shard_map/all_gather | solution.py:98
  35.6 0.0 copy-done
  35.6 2.1 %fusion = f32[16,32,256]{2,1,0:T(8,128)S(1)} fusion(bf16[16,32,2304]{2,1,0:T(8,128)(2,1)S(1)} %copy-done, bf16[2304,256]{0,1:T(8,128)(2,1)} %all-gather.2.cloned.1.call-done), kind=kOutput, calls=%fused_computation.1 | convolution fusion | flops 603979776 | bytes 4063232 | tf_op jit(solution)/shard_map/dot_general | solution.py:99
  37.7 1.3 %collective-permute-start = (f32[16,32,256]{2,1,0:T(8,128)S(1)}, f32[16,32,256]{2,1,0:T(8,128)S(1)}, u32[]{:S(2)}, u32[]{:S(2)}) collective-permute-start(f32[16,32,256]{2,1,0:T(8,128)S(1)} %fusion), channel_id=1, source_target_pairs={{0,1},{1,0},{2,3},{3,2},{4,5},{5,4},{6,7},{7,6},{8,9},{9,8},{10,11... | collective-permute-start | bytes 1572872 | tf_op jit(solution)/shard_map/ppermute | solution.py:19
  39.0 12.0 %collective-permute-done = f32[16,32,256]{2,1,0:T(8,128)S(1)} collective-permute-done((f32[16,32,256]{2,1,0:T(8,128)S(1)}, f32[16,32,256]{2,1,0:T(8,128)S(1)}, u32[]{:S(2)}, u32[]{:S(2)}) %collective-permute-start) | collective-permute-done | bytes 524320 | tf_op jit(solution)/shard_map/ppermute | solution.py:19
  51.0 0.1 add.291
  51.1 2.2 %collective-permute-start.1 = (f32[16,32,256]{2,1,0:T(8,128)S(1)}, f32[16,32,256]{2,1,0:T(8,128)S(1)}, u32[]{:S(2)}, u32[]{:S(2)}) collective-permute-start(f32[16,32,256]{2,1,0:T(8,128)S(1)} %add.291), channel_id=1, source_target_pairs={{0,2},{1,3},{2,0},{3,1},{4,6},{5,7},{6,4},{7,5},{8,10},{9,11},{10,... | collective-permute-start | bytes 1572872 | tf_op jit(solution)/shard_map/ppermute | solution.py:19
  53.2 0.0 copy-done.3
  53.3 4.4 %collective-permute-start.2 = (f32[3,32]{1,0:T(4,128)S(1)}, f32[3,32]{1,0:T(4,128)S(1)}, u32[]{:S(2)}, u32[]{:S(2)}) collective-permute-start(f32[3,32]{1,0:T(4,128)S(1)} %get-tuple-element.121), channel_id=1, source_target_pairs={{0,8},{8,16},{16,24},{1,9},{9,17},{17,25},{2,10},{10,18},{18,26},{... | collective-permute-start | bytes 1160 | tf_op jit(solution)/shard_map/ppermute | solution.py:40
  57.7 1.9 %collective-permute-start.3 = (f32[3,32]{1,0:T(4,128)S(1)}, f32[3,32]{1,0:T(4,128)S(1)}, u32[]{:S(2)}, u32[]{:S(2)}) collective-permute-start(f32[3,32]{1,0:T(4,128)S(1)} %get-tuple-element.122), channel_id=1, source_target_pairs={{8,0},{16,8},{24,16},{9,1},{17,9},{25,17},{10,2},{18,10},{26,18},{... | collective-permute-start | bytes 1160 | tf_op jit(solution)/shard_map/ppermute | solution.py:41
  59.6 0.0 collective-permute-done.2
  59.6 3.0 %collective-permute-done.3 = f32[3,32]{1,0:T(4,128)S(1)} collective-permute-done((f32[3,32]{1,0:T(4,128)S(1)}, f32[3,32]{1,0:T(4,128)S(1)}, u32[]{:S(2)}, u32[]{:S(2)}) %collective-permute-start.3) | collective-permute-done | bytes 416 | tf_op jit(solution)/shard_map/ppermute | solution.py:41
  62.6 13.6 %collective-permute-done.1 = f32[16,32,256]{2,1,0:T(8,128)S(1)} collective-permute-done((f32[16,32,256]{2,1,0:T(8,128)S(1)}, f32[16,32,256]{2,1,0:T(8,128)S(1)}, u32[]{:S(2)}, u32[]{:S(2)}) %collective-permute-start.1) | collective-permute-done | bytes 524320 | tf_op jit(solution)/shard_map/ppermute | solution.py:19
  76.2 0.1 add.292
  76.3 4.4 %collective-permute-start.5 = (f32[3,32,256]{2,1,0:T(8,128)S(1)}, f32[3,32,256]{2,1,0:T(8,128)S(1)}, u32[]{:S(2)}, u32[]{:S(2)}) collective-permute-start(f32[3,32,256]{2,1,0:T(8,128)S(1)} %get-tuple-element.115), channel_id=1, source_target_pairs={{0,8},{8,16},{16,24},{1,9},{9,17},{17,25},{2,10},{10,18},{18,26},{... | collective-permute-start | bytes 294920 | tf_op jit(solution)/shard_map/ppermute | solution.py:40
  80.7 1.9 %collective-permute-start.6 = (f32[3,32,256]{2,1,0:T(8,128)S(1)}, f32[3,32,256]{2,1,0:T(8,128)S(1)}, u32[]{:S(2)}, u32[]{:S(2)}) collective-permute-start(f32[3,32,256]{2,1,0:T(8,128)S(1)} %get-tuple-element.116), channel_id=1, source_target_pairs={{8,0},{16,8},{24,16},{9,1},{17,9},{25,17},{10,2},{18,10},{26,18},{... | collective-permute-start | bytes 294920 | tf_op jit(solution)/shard_map/ppermute | solution.py:41
  82.6 0.1 fusion.59
  82.7 1.3 %collective-permute-start.8 = (f32[22,3]{1,0:T(8,128)S(1)}, f32[22,3]{1,0:T(8,128)S(1)}, u32[]{:S(2)}, u32[]{:S(2)}) collective-permute-start(f32[22,3]{1,0:T(8,128)S(1)} %get-tuple-element.119), channel_id=1, source_target_pairs={{4,0},{5,1},{6,2},{7,3},{12,8},{13,9},{14,10},{15,11},{20,16},{21,... | collective-permute-start | bytes 800 | tf_op jit(solution)/shard_map/ppermute | solution.py:41
  84.0 4.0 %collective-permute-start.4 = (f32[22,3]{1,0:T(8,128)S(1)}, f32[22,3]{1,0:T(8,128)S(1)}, u32[]{:S(2)}, u32[]{:S(2)}) collective-permute-start(f32[22,3]{1,0:T(8,128)S(1)} %get-tuple-element.120), channel_id=1, source_target_pairs={{0,4},{1,5},{2,6},{3,7},{8,12},{9,13},{10,14},{11,15},{16,20},{17,... | collective-permute-start | bytes 800 | tf_op jit(solution)/shard_map/ppermute | solution.py:40
  88.0 0.0 collective-permute-done.5
  88.0 0.0 collective-permute-done.6
  88.0 1.3 %collective-permute-start.7 = (f32[22,3,256]{2,1,0:T(4,128)S(1)}, f32[22,3,256]{2,1,0:T(4,128)S(1)}, u32[]{:S(2)}, u32[]{:S(2)}) collective-permute-start(f32[22,3,256]{2,1,0:T(4,128)S(1)} %get-tuple-element.113), channel_id=1, source_target_pairs={{0,4},{1,5},{2,6},{3,7},{8,12},{9,13},{10,14},{11,15},{16,20},{17,... | collective-permute-start | bytes 202760 | tf_op jit(solution)/shard_map/ppermute | solution.py:40
  89.3 1.3 %collective-permute-start.9 = (f32[22,3,256]{2,1,0:T(4,128)S(1)}, f32[22,3,256]{2,1,0:T(4,128)S(1)}, u32[]{:S(2)}, u32[]{:S(2)}) collective-permute-start(f32[22,3,256]{2,1,0:T(4,128)S(1)} %get-tuple-element.114), channel_id=1, source_target_pairs={{4,0},{5,1},{6,2},{7,3},{12,8},{13,9},{14,10},{15,11},{20,16},{21,... | collective-permute-start | bytes 202760 | tf_op jit(solution)/shard_map/ppermute | solution.py:41
  90.6 0.0 collective-permute-done.8
  90.6 0.0 collective-permute-done.4
  90.6 0.1 pad_maximum_fusion.7
  90.7 0.1 collective-permute-done.7
  90.9 3.7 %collective-permute-done.9 = f32[22,3,256]{2,1,0:T(4,128)S(1)} collective-permute-done((f32[22,3,256]{2,1,0:T(4,128)S(1)}, f32[22,3,256]{2,1,0:T(4,128)S(1)}, u32[]{:S(2)}, u32[]{:S(2)}) %collective-permute-start.9) | collective-permute-done | bytes 67616 | tf_op jit(solution)/shard_map/ppermute | solution.py:41
  94.6 0.1 maximum_maximum_fusion
  94.7 1.9 %multiply_reduce_fusion.45 = (f32[16,32]{1,0:T(8,128)S(1)}, f32[16,32]{1,0:T(8,128)S(1)}, f32[16,32]{1,0:T(8,128)S(1)}, f32[16,32]{1,0:T(8,128)S(1)}, f32[16,32]...) fusion(f32[16,32,256]{2,1,0:T(8,128)S(1)} %add.292, ...), kind=kLoop, calls=%fused_computation.99 | loop fusion | flops 7068672 | bytes 9998336 | tf_op jit(solution)/shard_map/reduce_sum | solution.py:64
  96.6 2.1 %multiply_reduce_fusion.41 = (f32[16,32]{1,0:T(8,128)S(1)}, f32[16,32]{1,0:T(8,128)S(1)}, f32[16,32]{1,0:T(8,128)S(1)}, f32[16,32]{1,0:T(8,128)S(1)}, f32[16,32]...) fusion(f32[16,32,256]{2,1,0:T(8,128)S(1)} %add.292, ...), kind=kLoop, calls=%fused_computation.95 | loop fusion | flops 7068672 | bytes 9998336 | tf_op jit(solution)/shard_map/reduce_sum | solution.py:64
  98.7 0.0 copy-start.2
  98.7 1.1 multiply_reduce_fusion.44
  99.8 0.0 copy-done.2
  99.8 0.2 add_add_fusion
  100.0 0.0 copy-start.1
  100.0 5.3 %fusion.41 = bf16[16,32,256]{2,1,0:T(8,128)(2,1)S(1)} fusion(f32[3,32,256]{2,1,0:T(8,128)S(1)} %collective-permute-done.6, f32[16,32,256]{2,1,0:T(8,128)S(1)} %add.292, f32[3,32,256]{2,1,0:T(8,128)S(1)} %collective-permute-done.5, f32[22,35,256]{2,1,0:T(8,128)S(1)} %get-tuple-element.112, f32[22,35,256]{2,1,0:T(8,128)S(1)} %get-tuple-element.111, ...), kind=kLoop, calls=%fused_computation.100 | loop fusion | flops 13631488 | bytes 23103488 | tf_op jit(solution)/shard_map/convert_element_type | solution.py:105
  105.3 0.0 copy-done.1
  105.3 2.2 %convolution_convert_fusion = bf16[512,2304]{1,0:T(8,128)(2,1)} fusion(bf16[512,256]{1,0:T(8,128)(2,1)S(1)} %bitcast.8, bf16[2304,256]{0,1:T(8,128)(2,1)S(1)} %copy-done.1), kind=kOutput, calls=%fused_computation | convolution fusion | flops 605159424 | bytes 3801088 | tf_op jit(solution)/shard_map/dot_general | solution.py:107
  (5 shorter events, 0.1 us)
Async XLA Ops:
  6.5 29.1 %copy-start = (bf16[16,32,2304]{2,1,0:T(8,128)(2,1)S(1)}, bf16[16,32,2304]{2,1,0:T(8,128)(2,1)}, u32[]{:S(2)}) copy-start(bf16[16,32,2304]{2,1,0:T(8,128)(2,1)} %param.4) | copy-start | bytes 7077892
  6.5 29.1 %all-gather.2.cloned.1.call-start = ((), (), s32[]{:S(2)}) async-start(), calls=%async_computation | async-start | bytes 1327104 | tf_op jit(solution)/shard_map/all_gather | solution.py:98
  7.3 46.0 %copy-start.3 = (s32[16,32]{1,0:T(8,128)S(1)}, s32[16,32]{1,0:T(8,128)}, u32[]{:S(2)}) copy-start(s32[16,32]{1,0:T(8,128)} %param.6) | copy-start | bytes 6148
  37.7 13.3 %collective-permute-start = (f32[16,32,256]{2,1,0:T(8,128)S(1)}, f32[16,32,256]{2,1,0:T(8,128)S(1)}, u32[]{:S(2)}, u32[]{:S(2)}) collective-permute-start(f32[16,32,256]{2,1,0:T(8,128)S(1)} %fusion), channel_id=1, source_target_pairs={{0,1},{1,0},{2,3},{3,2},{4,5},{5,4},{6,7},{7,6},{8,9},{9,8},{10,11... | collective-permute-start | bytes 1572872 | tf_op jit(solution)/shard_map/ppermute | solution.py:19
  51.1 25.1 %collective-permute-start.1 = (f32[16,32,256]{2,1,0:T(8,128)S(1)}, f32[16,32,256]{2,1,0:T(8,128)S(1)}, u32[]{:S(2)}, u32[]{:S(2)}) collective-permute-start(f32[16,32,256]{2,1,0:T(8,128)S(1)} %add.291), channel_id=1, source_target_pairs={{0,2},{1,3},{2,0},{3,1},{4,6},{5,7},{6,4},{7,5},{8,10},{9,11},{10,... | collective-permute-start | bytes 1572872 | tf_op jit(solution)/shard_map/ppermute | solution.py:19
  53.3 6.3 %collective-permute-start.2 = (f32[3,32]{1,0:T(4,128)S(1)}, f32[3,32]{1,0:T(4,128)S(1)}, u32[]{:S(2)}, u32[]{:S(2)}) collective-permute-start(f32[3,32]{1,0:T(4,128)S(1)} %get-tuple-element.121), channel_id=1, source_target_pairs={{0,8},{8,16},{16,24},{1,9},{9,17},{17,25},{2,10},{10,18},{18,26},{... | collective-permute-start | bytes 1160 | tf_op jit(solution)/shard_map/ppermute | solution.py:40
  57.7 4.9 %collective-permute-start.3 = (f32[3,32]{1,0:T(4,128)S(1)}, f32[3,32]{1,0:T(4,128)S(1)}, u32[]{:S(2)}, u32[]{:S(2)}) collective-permute-start(f32[3,32]{1,0:T(4,128)S(1)} %get-tuple-element.122), channel_id=1, source_target_pairs={{8,0},{16,8},{24,16},{9,1},{17,9},{25,17},{10,2},{18,10},{26,18},{... | collective-permute-start | bytes 1160 | tf_op jit(solution)/shard_map/ppermute | solution.py:41
  76.3 11.7 %collective-permute-start.5 = (f32[3,32,256]{2,1,0:T(8,128)S(1)}, f32[3,32,256]{2,1,0:T(8,128)S(1)}, u32[]{:S(2)}, u32[]{:S(2)}) collective-permute-start(f32[3,32,256]{2,1,0:T(8,128)S(1)} %get-tuple-element.115), channel_id=1, source_target_pairs={{0,8},{8,16},{16,24},{1,9},{9,17},{17,25},{2,10},{10,18},{18,26},{... | collective-permute-start | bytes 294920 | tf_op jit(solution)/shard_map/ppermute | solution.py:40
  80.7 7.3 %collective-permute-start.6 = (f32[3,32,256]{2,1,0:T(8,128)S(1)}, f32[3,32,256]{2,1,0:T(8,128)S(1)}, u32[]{:S(2)}, u32[]{:S(2)}) collective-permute-start(f32[3,32,256]{2,1,0:T(8,128)S(1)} %get-tuple-element.116), channel_id=1, source_target_pairs={{8,0},{16,8},{24,16},{9,1},{17,9},{25,17},{10,2},{18,10},{26,18},{... | collective-permute-start | bytes 294920 | tf_op jit(solution)/shard_map/ppermute | solution.py:41
  82.7 8.0 %collective-permute-start.8 = (f32[22,3]{1,0:T(8,128)S(1)}, f32[22,3]{1,0:T(8,128)S(1)}, u32[]{:S(2)}, u32[]{:S(2)}) collective-permute-start(f32[22,3]{1,0:T(8,128)S(1)} %get-tuple-element.119), channel_id=1, source_target_pairs={{4,0},{5,1},{6,2},{7,3},{12,8},{13,9},{14,10},{15,11},{20,16},{21,... | collective-permute-start | bytes 800 | tf_op jit(solution)/shard_map/ppermute | solution.py:41
  84.0 6.7 %collective-permute-start.4 = (f32[22,3]{1,0:T(8,128)S(1)}, f32[22,3]{1,0:T(8,128)S(1)}, u32[]{:S(2)}, u32[]{:S(2)}) collective-permute-start(f32[22,3]{1,0:T(8,128)S(1)} %get-tuple-element.120), channel_id=1, source_target_pairs={{0,4},{1,5},{2,6},{3,7},{8,12},{9,13},{10,14},{11,15},{16,20},{17,... | collective-permute-start | bytes 800 | tf_op jit(solution)/shard_map/ppermute | solution.py:40
  88.0 2.8 %collective-permute-start.7 = (f32[22,3,256]{2,1,0:T(4,128)S(1)}, f32[22,3,256]{2,1,0:T(4,128)S(1)}, u32[]{:S(2)}, u32[]{:S(2)}) collective-permute-start(f32[22,3,256]{2,1,0:T(4,128)S(1)} %get-tuple-element.113), channel_id=1, source_target_pairs={{0,4},{1,5},{2,6},{3,7},{8,12},{9,13},{10,14},{11,15},{16,20},{17,... | collective-permute-start | bytes 202760 | tf_op jit(solution)/shard_map/ppermute | solution.py:40
  89.3 5.3 %collective-permute-start.9 = (f32[22,3,256]{2,1,0:T(4,128)S(1)}, f32[22,3,256]{2,1,0:T(4,128)S(1)}, u32[]{:S(2)}, u32[]{:S(2)}) collective-permute-start(f32[22,3,256]{2,1,0:T(4,128)S(1)} %get-tuple-element.114), channel_id=1, source_target_pairs={{4,0},{5,1},{6,2},{7,3},{12,8},{13,9},{14,10},{15,11},{20,16},{21,... | collective-permute-start | bytes 202760 | tf_op jit(solution)/shard_map/ppermute | solution.py:41
  98.7 1.1 copy-start.2
  100.0 5.3 %copy-start.1 = (bf16[2304,256]{0,1:T(8,128)(2,1)S(1)}, bf16[2304,256]{0,1:T(8,128)(2,1)}, u32[]{:S(2)}) copy-start(bf16[2304,256]{0,1:T(8,128)(2,1)} %all-gather.2.cloned.1.call-done) | copy-start | bytes 3538948
Sparse Core Ops, SparseCore 0:
  9.2 26.3 all-gather.1
